TPU v7x, 256 devices: a whole 4x4x8 slice. The times are simulated.
256 devices in a mesh: gx: 8 (over y, x_hi), gy: 32 (over z, x_lo, core).
Axes of the slice: x: 4 (x_hi: 2, x_lo: 2; x = x_hi * 2 + x_lo), y: 4, z: 8, core: 2. Of those that a mesh axis runs over, the one named last changes fastest.
Arguments:
- species_means: bfloat16 [8, 64, 120, 1024], P(None, 'gy', None, 'gx'), may hold values from 0.19921875 to 5
- zonal_edge_velocity: float32 [64, 120, 1024], P('gy', None, 'gx'), may hold values from -6 to 6
- meridional_edge_velocity: float32 [64, 120, 1024], P('gy', None, 'gx'), may hold values from -6 to 6
- scaled_warmth: float32 [64, 120, 1024], P('gy', None, 'gx'), may hold values from 0.5 to 2
- donor_depths: float32 [64, 120, 1024], P('gy', None, 'gx'), may hold values from 0.5 to 2
- leading_donor_level: int32 [64, 120, 1024], P('gy', None, 'gx'), may hold values from 0 to 118, as said below
- opening_share: bfloat16 [64, 120, 1024], P('gy', None, 'gx'), may hold values from 0 to 0.44921875
- closing_share: bfloat16 [64, 120, 1024], P('gy', None, 'gx'), may hold values from 0.546875 to 1
Outputs:
- tracers_out: float32 [8, 64, 120, 1024], P(None, 'gy', None, 'gx')
- regridded_zonal: float32 [64, 120, 1024], P('gy', None, 'gx')
- regridded_meridional: float32 [64, 120, 1024], P('gy', None, 'gx')
- adjusted_warmth: float32 [64, 120, 1024], P('gy', None, 'gx')
Inputs may be any that keep to these rules, and one draw needn't show every extreme that they name: Target layer k draws on source layers leading_donor_level and leading_donor_level + 1, and leading_donor_level lies within 2 of k.
All inputs are finite; a program needn't handle non-finite values.
Results may differ from a plain program's by a relative error of at most 0.0003.
Values sent between devices are 32-bit elements; how exact they have to be, the bound alone decides.
No kernel may reach another device: no remote copies, remote signals or barrier semaphores. Data moves between devices by JAX's collectives and lax.ppermute only.
A program may use at most 64 MiB of HBM per device.

v0:
```python
import jax
import jax.numpy as jnp
from jax import lax
from jax.sharding import Mesh
from jax.sharding import PartitionSpec as P

GY = ("gy_0", "gy_1", "gy_2")
GX = ("gx_0", "gx_1")
GX_GY = ("gx_0", "gx_1", "gy_0", "gy_1", "gy_2")
thermal_rescale_factor = 3.5
offsets_all = (-2, -1, 0, 1, 2, 3)


def passed_along(value, axis, steps):
    count = lax.axis_size(axis)
    pairs = [(source, (source + steps) % count) for source in range(count)]
    return lax.ppermute(value, axis, pairs)


def over_axes(x, axes):
    for axis in axes:
        x = lax.psum(x, axis)
    return x


def ppm_parts(values):
    layers = values.shape[-2]
    top_edge = 1.5 * values[..., 0:1, :] - 0.5 * values[..., 1:2, :]
    second_edge = 0.5 * (values[..., 0:1, :] + values[..., 1:2, :])
    inner_edge = 7.0 / 12.0 * (
        values[..., 1 : layers - 2, :] + values[..., 2 : layers - 1, :]
    ) - 1.0 / 12.0 * (values[..., 0 : layers - 3, :] + values[..., 3:layers, :])
    lower_edge = 0.5 * (
        values[..., layers - 2 : layers - 1, :] + values[..., layers - 1 : layers, :]
    )
    bottom_edge = (
        1.5 * values[..., layers - 1 : layers, :] - 0.5 * values[..., layers - 2 : layers - 1, :]
    )
    edge_values = jnp.concatenate(
        [top_edge, second_edge, inner_edge, lower_edge, bottom_edge], axis=-2
    )
    left_edge = edge_values[..., :layers, :]
    right_edge = edge_values[..., 1:, :]
    return (left_edge, right_edge - left_edge, 6.0 * values - 3.0 * (left_edge + right_edge))


def shifted_layers(values, amount):
    layers = values.shape[-2]
    if amount == 0:
        return values
    if amount > 0:
        filler = jnp.zeros(values.shape[:-2] + (amount, values.shape[-1]), values.dtype)
        return jnp.concatenate([values[..., amount:, :], filler], axis=-2)
    filler = jnp.zeros(values.shape[:-2] + (-amount, values.shape[-1]), values.dtype)
    return jnp.concatenate([filler, values[..., : layers + amount, :]], axis=-2)


def pick_layers(values, masks):
    total = jnp.zeros(values.shape, jnp.float32)
    for amount, selector in zip(offsets_all, masks):
        total = total + jnp.where(selector, shifted_layers(values, amount), 0.0)
    return total


def build_operator(donor_depths, leading_donor_level, opening_share, closing_share):
    start_frac = opening_share.astype(jnp.float32)
    end_frac = closing_share.astype(jnp.float32)
    layer_offset = leading_donor_level - lax.broadcasted_iota(
        jnp.int32, leading_donor_level.shape, 1
    )
    first_masks = [layer_offset == amount for amount in offsets_all]
    second_masks = [layer_offset + 1 == amount for amount in offsets_all]
    weight_first = (1.0 - start_frac) * pick_layers(donor_depths, first_masks)
    weight_second = end_frac * pick_layers(donor_depths, second_masks)
    linear_first = 0.5 * (start_frac + 1.0)
    square_first = linear_first - (start_frac * start_frac + start_frac + 1.0) / 3.0
    linear_second = 0.5 * end_frac
    square_second = linear_second - end_frac * end_frac / 3.0
    return (
        first_masks,
        second_masks,
        weight_first,
        weight_second,
        linear_first,
        square_first,
        linear_second,
        square_second,
    )


def multiply_by_regrid_operator(operator, values):
    (
        first_masks,
        second_masks,
        weight_first,
        weight_second,
        linear_first,
        square_first,
        linear_second,
        square_second,
    ) = operator
    left_edge, edge_slope, curvature = ppm_parts(values)
    mean_first = (
        pick_layers(left_edge, first_masks)
        + pick_layers(edge_slope, first_masks) * linear_first
        + pick_layers(curvature, first_masks) * square_first
    )
    mean_second = (
        pick_layers(left_edge, second_masks)
        + pick_layers(edge_slope, second_masks) * linear_second
        + pick_layers(curvature, second_masks) * square_second
    )
    return (weight_first * mean_first + weight_second * mean_second) / (
        weight_first + weight_second
    )


def local(
    species_means,
    zonal_edge_velocity,
    meridional_edge_velocity,
    scaled_warmth,
    donor_depths,
    leading_donor_level,
    opening_share,
    closing_share,
):
    vertical_regrid_operator = build_operator(
        donor_depths, leading_donor_level, opening_share, closing_share
    )
    regridded_depths = vertical_regrid_operator[2] + vertical_regrid_operator[3]
    mass_before = jnp.sum(species_means.astype(jnp.float32) * donor_depths, axis=(1, 2, 3))
    interior_u_faces = 0.5 * jnp.sum(
        0.5
        * (donor_depths[:-1] + donor_depths[1:])
        * zonal_edge_velocity[:-1]
        * zonal_edge_velocity[:-1]
    )
    interior_v_faces = 0.5 * jnp.sum(
        0.5
        * (donor_depths[:, :, :-1] + donor_depths[:, :, 1:])
        * meridional_edge_velocity[:, :, :-1]
        * meridional_edge_velocity[:, :, :-1]
    )
    local_prior_totals = (
        thermal_rescale_factor * jnp.sum(donor_depths * scaled_warmth)
        + interior_u_faces
        + interior_v_faces
    )
    from_south = passed_along(zonal_edge_velocity[-1:], GY, 1)
    u_paired = multiply_by_regrid_operator(
        vertical_regrid_operator,
        jnp.stack(
            [zonal_edge_velocity, jnp.concatenate([from_south, zonal_edge_velocity[:-1]], axis=0)]
        ),
    )
    u_cross = u_paired[1]
    returned = passed_along(
        jnp.stack([u_cross[0:1], donor_depths[0:1], regridded_depths[0:1]]), GY, -1
    )
    north_thick = returned[2]
    edge_u = 0.5 * jnp.sum(
        0.5
        * (donor_depths[-1:] + returned[1])
        * zonal_edge_velocity[-1:]
        * zonal_edge_velocity[-1:]
    )
    regridded_zonal = 0.5 * (u_paired[0] + jnp.concatenate([u_cross[1:], returned[0]], axis=0))
    zonal_following = 0.5 * jnp.sum(
        0.5
        * (regridded_depths + jnp.concatenate([regridded_depths[1:], north_thick], axis=0))
        * regridded_zonal
        * regridded_zonal
    )
    from_west = passed_along(meridional_edge_velocity[:, :, -1:], GX, 1)
    v_paired = multiply_by_regrid_operator(
        vertical_regrid_operator,
        jnp.stack(
            [
                meridional_edge_velocity,
                jnp.concatenate([from_west, meridional_edge_velocity[:, :, :-1]], axis=2),
            ]
        ),
    )
    v_cross = v_paired[1]
    v_returned = passed_along(
        jnp.stack([v_cross[:, :, 0:1], donor_depths[:, :, 0:1], regridded_depths[:, :, 0:1]]),
        GX,
        -1,
    )
    regridded_meridional = 0.5 * (
        v_paired[0] + jnp.concatenate([v_cross[:, :, 1:], v_returned[0]], axis=2)
    )
    edge_v = 0.5 * jnp.sum(
        0.5
        * (donor_depths[:, :, -1:] + v_returned[1])
        * meridional_edge_velocity[:, :, -1:]
        * meridional_edge_velocity[:, :, -1:]
    )
    meridional_following = 0.5 * jnp.sum(
        0.5
        * (regridded_depths + jnp.concatenate([regridded_depths[:, :, 1:], v_returned[2]], axis=2))
        * regridded_meridional
        * regridded_meridional
    )
    tracer_new = multiply_by_regrid_operator(
        vertical_regrid_operator, species_means.astype(jnp.float32)
    )
    regridded_warmth = multiply_by_regrid_operator(vertical_regrid_operator, scaled_warmth)
    mass_after = jnp.sum(tracer_new * regridded_depths, axis=(1, 2, 3))
    aggregate_regridded = jnp.sum(regridded_depths)
    kinetic_thermal_following = (
        thermal_rescale_factor * jnp.sum(regridded_depths * regridded_warmth)
        + zonal_following
        + meridional_following
    )
    mass_total_before, mass_total_after, scalars = (
        over_axes(mass_before, GX_GY),
        over_axes(mass_after, GX_GY),
        over_axes(
            jnp.stack(
                [
                    local_prior_totals + edge_u + edge_v,
                    kinetic_thermal_following,
                    aggregate_regridded,
                ]
            ),
            GX_GY,
        ),
    )
    enthalpy_global_preceding = scalars[0]
    enthalpy_global_following = scalars[1]
    thick_total = scalars[2]
    tracers_out = (
        tracer_new + ((mass_total_before - mass_total_after) / thick_total)[:, None, None, None]
    )
    adjusted_warmth = regridded_warmth + (enthalpy_global_preceding - enthalpy_global_following) / (
        thermal_rescale_factor * thick_total
    )
    return (tracers_out, regridded_zonal, regridded_meridional, adjusted_warmth)


def solution(mesh):
    split = Mesh(mesh.devices.reshape(4, 2, 8, 2, 2), ("gx_0", "gx_1", "gy_0", "gy_1", "gy_2"))
    in_specs = (
        P(None, GY, None, GX),
        P(GY, None, GX),
        P(GY, None, GX),
        P(GY, None, GX),
        P(GY, None, GX),
        P(GY, None, GX),
        P(GY, None, GX),
        P(GY, None, GX),
    )
    out_specs = (P(None, GY, None, GX), P(GY, None, GX), P(GY, None, GX), P(GY, None, GX))
    return jax.shard_map(local, mesh=split, in_specs=in_specs, out_specs=out_specs, check_vma=False)
```

profile of v0, /device:TPU:1, one launch (start us, length us, event | category | flops | bytes accessed | tf_op | source)
XLA Modules:
  0.0 101.0 jit_solution(2955615427944298031)
XLA Ops:
  0.6 1.7 %slice.551 = f32[2,120,1]{2,1,0:T(8,128)} slice(f32[2,120,128]{2,1,0:T(8,128)} %param.10), slice={[0:2], [0:120], [127:128]} | slice | bytes 1920 | tf_op jit(solution)/shard_map/slice | solution.py:175
  2.3 3.6 %collective-permute-start.2 = (f32[2,120,1]{2,1,0:T(8,128)}, f32[2,120,1]{2,1,0:T(8,128)S(1)}, u32[]{:S(2)}, u32[]{:S(2)}) collective-permute-start(f32[2,120,1]{2,1,0:T(8,128)} %slice.551), channel_id=1, source_target_pairs={{0,32},{32,64},{64,96},{96,128},{128,160},{160,192},{192,224},{224... | collective-permute-start | bytes 2888 | tf_op jit(solution)/shard_map/ppermute | solution.py:17
  5.9 0.6 fusion.103
  6.5 1.2 %collective-permute-start = (f32[1,120,128]{2,1,0:T(8,128)}, f32[1,120,128]{2,1,0:T(8,128)}, u32[]{:S(2)}, u32[]{:S(2)}) collective-permute-start(f32[1,120,128]{2,1,0:T(8,128)} %get-tuple-element.129), channel_id=1, source_target_pairs={{0,1},{1,2},{2,3},{3,4},{4,5},{5,6},{6,7},{7,8},{8,9},{9,10},{10,1... | collective-permute-start | bytes 184328 | tf_op jit(solution)/shard_map/ppermute | solution.py:17
  7.8 1.0 copy-done.2
  8.8 0.4 fusion.5
  9.2 0.6 fusion.7
  9.8 0.1 slice.631
  9.8 0.4 fusion.86
  10.2 0.4 fusion.87
  10.6 0.1 slice.626
  10.6 0.1 fusion
  10.7 0.1 pad_maximum_fusion.2
  10.8 0.1 pad_maximum_fusion.3
  10.9 0.8 copy-done.1
  11.7 0.7 fusion.46
  12.4 0.1 copy-done.12
  12.6 0.1 copy-done.15
  12.7 0.4 fusion.51
  13.1 0.1 slice_reduce_fusion
  13.2 0.7 fusion.102
  13.9 0.3 copy-done.3
  14.3 0.7 fusion.61
  15.0 0.8 fusion.98
  15.7 0.8 fusion.99
  16.5 0.7 fusion.40
  17.2 0.7 pad_maximum_fusion.20
  17.9 7.7 %multiply_reduce_fusion = (f32[8]{0:T(128)S(1)}, f32[8,2,120,128]{3,2,1,0:T(8,128)S(1)}) fusion(f32[2,120,128]{2,1,0:T(8,128)S(1)} %get-tuple-element.137, f32[2,120,128]{2,1,0:T(8,128)S(1)} %get-tuple-element.153, f32[2,120,128]{2,1,0:T(8,128)S(1)} %get-tuple-element.152, pred[2,120,128]{2,1,0:T(8,128)(4,1)S(1)} %get-tuple-element.139, ...), kind=kLoop, calls=%fused_computation.18 | loop fusion | flops 24084472 | bytes 17244192 | tf_op jit(solution)/shard_map/reduce_sum | solution.py:210
  25.6 0.8 slice.715
  26.4 0.7 slice.709
  27.1 0.7 slice.704
  29.0 0.1 maximum_bitcast_fusion.1
  29.2 0.1 fusion.19
  29.3 0.1 fusion.38
  29.7 1.0 add_divide_fusion.1
  30.7 0.1 slice_reduce_fusion.1
  30.8 0.8 slice.718
  31.6 3.8 %collective-permute-start.3 = (f32[3,2,120,1]{2,1,3,0:T(2,128)S(1)}, f32[3,2,120,1]{2,1,3,0:T(2,128)S(1)}, u32[]{:S(2)}, u32[]{:S(2)}) collective-permute-start(f32[3,2,120,1]{2,1,3,0:T(2,128)S(1)} %pad_maximum_fusion.23), channel_id=1, source_target_pairs={{0,224},{32,0},{64,32},{96,64},{128,96},{160,128},{192,160},{224,1... | collective-permute-start | bytes 8648 | tf_op jit(solution)/shard_map/ppermute | solution.py:17
  35.4 0.8 maximum_bitcast_fusion
  36.3 0.1 fusion.30
  36.4 0.1 fusion.39
  36.8 1.0 add_divide_fusion.2
  37.8 0.6 slice_bitcast_fusion.4
  38.5 0.2 copy-done.11
  38.7 0.7 pad_maximum_fusion.17
  39.4 0.3 collective-permute-start.1
  39.6 0.8 copy.187
  40.4 0.8 copy.188
  41.2 0.1 copy.180
  41.4 0.7 fusion.47
  42.7 2.0 %collective-permute-done.1 = f32[3,1,120,128]{3,2,1,0:T(8,128)} collective-permute-done((f32[3,1,120,128]{3,2,1,0:T(8,128)}, f32[3,1,120,128]{3,2,1,0:T(8,128)}, u32[]{:S(2)}, u32[]{:S(2)}) %collective-permute-start.1) | collective-permute-done | bytes 184352 | tf_op jit(solution)/shard_map/ppermute | solution.py:17
  44.6 0.9 slice_bitcast_fusion.3
  45.6 3.6 %fusion.49 = (f32[]{:T(128)}, f32[]{:T(128)}, f32[]{:T(128)}, f32[]{:T(128)}, f32[2,120,128]{2,1,0:T(8,128)}, /*index=5*/f32[2,120,128]{2,1,0:T(8,128)}, f32[2,120,128]{2,1,0:T(8,128)}) fusion(f32[2,120,128]{2,1,0:T(8,128)S(1)} %get-tuple-element.137, f32[2,120,1]{2,1,0:T(8,128)} %copy.187, f32[2,120,127]{2,1,0:T(8,128)} %slice.715, ...), kind=kLoop, calls=%fused_computation.136 | loop fusion | flops 3839996 | bytes 3906576 | tf_op jit(solution)/shard_map/reduce_sum | solution.py:200
  51.1 1.5 %fusion.63 = (f32[]{:T(128)}, f32[]{:T(128)}) fusion(f32[3,1,120,128]{3,2,1,0:T(8,128)} %collective-permute-done.1, f32[2,120,128]{2,1,0:T(8,128)S(1)} %copy-done, f32[2,120,128]{2,1,0:T(8,128)S(1)} %copy-done.4), kind=kLoop, calls=%fused_computation.176 | loop fusion | flops 153598 | bytes 307208 | tf_op jit(solution)/shard_map/reduce_sum | solution.py:162
  53.9 0.7 pad_maximum_fusion.24
  54.6 7.5 %all-reduce.66 = (f32[8]{0:T(128)S(1)}, f32[8]{0:T(128)S(1)}, f32[3]{0:T(128)S(1)}) all-reduce(f32[8]{0:T(128)S(1)} %get-tuple-element.79, f32[8]{0:T(128)S(1)} %get-tuple-element.48, f32[3]{0:T(128)S(1)} %pad_maximum_fusion.24), channel_id=1, replica_groups=mesh['gx_0'=4,'gx_1'=2,'gy_0'=8,'gy_1'=2,'gy_2'=2] {'gx_0'}, use_global_device_ids=true, to_apply=%region_1.2 | all-reduce | flops 19 | bytes 152 | tf_op jit(solution)/shard_map/psum | solution.py:22
  62.1 5.3 %all-reduce.69 = (f32[8]{0:T(128)S(1)}, f32[8]{0:T(128)S(1)}, f32[3]{0:T(128)S(1)}) all-reduce(f32[8]{0:T(128)S(1)} %get-tuple-element.21, f32[8]{0:T(128)S(1)} %get-tuple-element.22, f32[3]{0:T(128)S(1)} %get-tuple-element.23), channel_id=1, replica_groups=mesh['gx_0'=4,'gx_1'=2,'gy_0'=8,'gy_1'=2,'gy_2'=2] {'gx_1'}, use_global_device_ids=true, to_apply=%region_2.3 | all-reduce | flops 19 | bytes 152 | tf_op jit(solution)/shard_map/psum | solution.py:22
  67.3 16.3 %all-reduce.65 = (f32[8]{0:T(128)S(1)}, f32[8]{0:T(128)S(1)}, f32[3]{0:T(128)S(1)}) all-reduce(f32[8]{0:T(128)S(1)} %get-tuple-element.30, f32[8]{0:T(128)S(1)} %get-tuple-element.31, f32[3]{0:T(128)S(1)} %get-tuple-element.32), channel_id=1, replica_groups=mesh['gx_0'=4,'gx_1'=2,'gy_0'=8,'gy_1'=2,'gy_2'=2] {'gy_0'}, use_global_device_ids=true, to_apply=%region_3.4 | all-reduce | flops 19 | bytes 152 | tf_op jit(solution)/shard_map/psum | solution.py:22
  83.6 3.8 %all-reduce.68 = (f32[8]{0:T(128)S(1)}, f32[8]{0:T(128)S(1)}, f32[3]{0:T(128)S(1)}) all-reduce(f32[8]{0:T(128)S(1)} %get-tuple-element.18, f32[8]{0:T(128)S(1)} %get-tuple-element.19, f32[3]{0:T(128)S(1)} %get-tuple-element.20), channel_id=1, replica_groups=mesh['gx_0'=4,'gx_1'=2,'gy_0'=8,'gy_1'=2,'gy_2'=2] {'gy_1'}, use_global_device_ids=true, to_apply=%region_4.5 | all-reduce | flops 19 | bytes 152 | tf_op jit(solution)/shard_map/psum | solution.py:22
  87.4 8.6 %all-reduce.67 = (f32[8]{0:T(128)S(1)}, f32[8]{0:T(128)S(1)}, f32[3]{0:T(128)S(1)}) all-reduce(f32[8]{0:T(128)S(1)} %get-tuple-element.27, f32[8]{0:T(128)S(1)} %get-tuple-element.28, f32[3]{0:T(128)S(1)} %get-tuple-element.29), channel_id=1, replica_groups=mesh['gx_0'=4,'gx_1'=2,'gy_0'=8,'gy_1'=2,'gy_2'=2] {'gy_2'}, use_global_device_ids=true, to_apply=%region_5.6 | all-reduce | flops 19 | bytes 152 | tf_op jit(solution)/shard_map/psum | solution.py:22
  95.9 0.6 fusion.106
  97.2 0.7 subtract_divide_fusion
  97.9 1.1 %broadcast_add_fusion = f32[8,2,120,128]{3,2,1,0:T(8,128)} fusion(f32[8,2,120,128]{3,2,1,0:T(8,128)S(1)} %get-tuple-element.49, f32[8]{0:T(128)S(1)} %subtract_divide_fusion), kind=kLoop, calls=%fused_computation.57 | loop fusion | flops 245760 | bytes 1966112 | tf_op jit(solution)/shard_map/add | solution.py:235
  100.3 0.7 broadcast_add_fusion.1
  (66 shorter events, 1.0 us)
Async XLA Ops:
  0.6 5.3 %copy-start.4 = (f32[2,120,128]{2,1,0:T(8,128)S(1)}, f32[2,120,128]{2,1,0:T(8,128)}, u32[]{:S(2)}) copy-start(f32[2,120,128]{2,1,0:T(8,128)} %param.9) | copy-start | bytes 368644
  2.3 5.4 %copy-start = (f32[2,120,128]{2,1,0:T(8,128)S(1)}, f32[2,120,128]{2,1,0:T(8,128)}, u32[]{:S(2)}) copy-start(f32[2,120,128]{2,1,0:T(8,128)} %param.12) | copy-start | bytes 368644
  2.3 26.7 %collective-permute-start.2 = (f32[2,120,1]{2,1,0:T(8,128)}, f32[2,120,1]{2,1,0:T(8,128)S(1)}, u32[]{:S(2)}, u32[]{:S(2)}) collective-permute-start(f32[2,120,1]{2,1,0:T(8,128)} %slice.551), channel_id=1, source_target_pairs={{0,32},{32,64},{64,96},{96,128},{128,160},{160,192},{192,224},{224... | collective-permute-start | bytes 2888 | tf_op jit(solution)/shard_map/ppermute | solution.py:17
  6.5 28.9 %collective-permute-start = (f32[1,120,128]{2,1,0:T(8,128)}, f32[1,120,128]{2,1,0:T(8,128)}, u32[]{:S(2)}, u32[]{:S(2)}) collective-permute-start(f32[1,120,128]{2,1,0:T(8,128)} %get-tuple-element.129), channel_id=1, source_target_pairs={{0,1},{1,2},{2,3},{3,4},{4,5},{5,6},{6,7},{7,8},{8,9},{9,10},{10,1... | collective-permute-start | bytes 184328 | tf_op jit(solution)/shard_map/ppermute | solution.py:17
  7.7 1.0 %copy-start.2 = (bf16[8,2,120,128]{3,2,1,0:T(8,128)(2,1)S(1)}, bf16[8,2,120,128]{3,2,1,0:T(8,128)(2,1)}, u32[]{:S(2)}) copy-start(bf16[8,2,120,128]{3,2,1,0:T(8,128)(2,1)} %param.8) | copy-start | bytes 1474564
  10.8 0.9 copy-start.1
  11.7 0.8 copy-start.12
  11.7 0.9 copy-start.13
  11.7 1.0 copy-start.15
  13.2 1.0 copy-start.3
  31.6 8.0 %collective-permute-start.3 = (f32[3,2,120,1]{2,1,3,0:T(2,128)S(1)}, f32[3,2,120,1]{2,1,3,0:T(2,128)S(1)}, u32[]{:S(2)}, u32[]{:S(2)}) collective-permute-start(f32[3,2,120,1]{2,1,3,0:T(2,128)S(1)} %pad_maximum_fusion.23), channel_id=1, source_target_pairs={{0,224},{32,0},{64,32},{96,64},{128,96},{160,128},{192,160},{224,1... | collective-permute-start | bytes 8648 | tf_op jit(solution)/shard_map/ppermute | solution.py:17
  37.8 0.8 copy-start.11
  39.4 5.3 %collective-permute-start.1 = (f32[3,1,120,128]{3,2,1,0:T(8,128)}, f32[3,1,120,128]{3,2,1,0:T(8,128)}, u32[]{:S(2)}, u32[]{:S(2)}) collective-permute-start(f32[3,1,120,128]{3,2,1,0:T(8,128)} %pad_maximum_fusion.17), channel_id=1, source_target_pairs={{0,31},{1,0},{2,1},{3,2},{4,3},{5,4},{6,5},{7,6},{8,7},{9,8},{10,9... | collective-permute-start | bytes 552968 | tf_op jit(solution)/shard_map/ppermute | solution.py:17
  40.4 5.1 %copy-start.7 = (f32[2,118,128]{2,1,0:T(8,128)S(1)}, f32[2,118,128]{2,1,0:T(8,128)}, u32[]{:S(2)}) copy-start(f32[2,118,128]{2,1,0:T(8,128)} %get-tuple-element.168) | copy-start | bytes 362500
  40.4 5.1 %copy-start.8 = (f32[2,118,128]{2,1,0:T(8,128)S(1)}, f32[2,118,128]{2,1,0:T(8,128)}, u32[]{:S(2)}) copy-start(f32[2,118,128]{2,1,0:T(8,128)} %get-tuple-element.169) | copy-start | bytes 362500
  40.4 5.1 %copy-start.14 = (f32[1,120,128]{2,1,0:T(8,128)S(1)}, f32[1,120,128]{2,1,0:T(8,128)}, u32[]{:S(2)}) copy-start(f32[1,120,128]{2,1,0:T(8,128)} %get-tuple-element.127) | copy-start | bytes 184324
  41.2 4.3 %copy-start.9 = (f32[2,119,128]{2,1,0:T(8,128)S(1)}, f32[2,119,128]{2,1,0:T(8,128)}, u32[]{:S(2)}) copy-start(f32[2,119,128]{2,1,0:T(8,128)} %get-tuple-element.121) | copy-start | bytes 365572
  42.6 2.9 %copy-start.5 = (f32[2,118,128]{2,1,0:T(8,128)S(1)}, f32[2,118,128]{2,1,0:T(8,128)}, u32[]{:S(2)}) copy-start(f32[2,118,128]{2,1,0:T(8,128)} %get-tuple-element.119) | copy-start | bytes 362500
  42.7 2.9 %copy-start.6 = (f32[2,118,128]{2,1,0:T(8,128)S(1)}, f32[2,118,128]{2,1,0:T(8,128)}, u32[]{:S(2)}) copy-start(f32[2,118,128]{2,1,0:T(8,128)} %get-tuple-element.120) | copy-start | bytes 362500
  97.8 2.5 %copy-start.10 = (f32[2,120,128]{2,1,0:T(8,128)S(1)}, f32[2,120,128]{2,1,0:T(8,128)}, u32[]{:S(2)}) copy-start(f32[2,120,128]{2,1,0:T(8,128)} %get-tuple-element.33) | copy-start | bytes 368644
where the time goes:
time: 102 us; the launch traced here: 101 us
  blocking collectives  41.4 us (41%)
  other arithmetic  25.3 us (25%)
  local copies, waits for them, and re-layouts  15.3 us (15%)
  starting transfers between devices  8.84 us (9%)
  between operations  8.16 us (8%)
  waiting for transfers between devices  1.97 us (2%)
    psum x5, blocking collectives, over_axes(): x = lax.psum(x, axis)  41.4 us
    ppermute x4, starting transfers between devices, passed_along(): return lax.ppermute(value, axis, pairs)  8.84 us
    reduce_sum x1, other arithmetic, local(): mass_after = jnp.sum(tracer_new * regridded_depths, axis=(1, 2, 3))  7.73 us
    reduce_sum x1, other arithmetic, local(): jnp.sum(0.5 * (regridded_depths + jnp.concatenate([regridded_depths[:, :,...  3.63 us
    slice x14, local copies, waits for them, and re-layouts, shifted_layers(): return jnp.concatenate([filler, values[..., :layers + amount, :]], axis=-2)  2.61 us
    unnamed x33, local copies, waits for them, and re-layouts  2.61 us
  transfers between devices with their start and end apart: 4, of which 1 were waited for; matrix products, arithmetic and copies ran while one was open for 26% of the time, Pallas kernels for 0%

commit v1 on v0

--- a/solution.py
+++ b/solution.py
@@ -19,7 +19,8 @@
 
 def over_axes(x, axes):
     for axis in axes:
-        x = lax.psum(x, axis)
+        parts = lax.all_gather(x, axis)
+        x = jnp.sum(parts, axis=0)
     return x
 
 

time: 102 us -> 136 us (1.33)
  local copies, waits for them, and re-layouts: 15.3 us -> 35.6 us
  between operations: 8.16 us -> 15.2 us
  other arithmetic: 25.3 us -> 31.9 us
    unnamed x0 -> x5, blocking collectives: none -> 41.5 us
    psum x5 -> x0, blocking collectives: 41.4 us -> none  [over_axes(): x = lax.psum(x, axis)]
    unnamed x33 -> x157, local copies, waits for them, and re-layouts: 2.61 us -> 16.1 us
    slice x14, local copies, waits for them, and re-layouts: 2.61 us -> 5.98 us  [shifted_layers(): return jnp.concatenate([filler, values[..., :layers + amount, :]], axis=-2)]
    concatenate x12, other arithmetic: 1.74 us -> 4.34 us  [ppm_parts(): jnp.concatenate([top_edge, second_edge, inner_edge, lower_edge, bottom_ed...]
    slice x9, local copies, waits for them, and re-layouts: 1.56 us -> 3.48 us  [shifted_layers(): return jnp.concatenate([values[..., amount:, :], filler], axis=-2)]
  transfers between devices with their start and end apart: 4 -> 4, of which waited for: 1 -> 1; matrix products, arithmetic and copies ran while one was open for 26% -> 34% of each run, Pallas kernels for 0% -> 0%
where the time goes in v1:
time: 136 us; the launch traced here: 135 us
  blocking collectives  41.5 us (31%)
  local copies, waits for them, and re-layouts  35.6 us (26%)
  other arithmetic  31.9 us (23%)
  between operations  15.2 us (11%)
  starting transfers between devices  8.92 us (7%)
  waiting for transfers between devices  1.47 us (1%)
    unnamed x5, blocking collectives  41.5 us
    unnamed x157, local copies, waits for them, and re-layouts  16.1 us
    reduce_sum x1, other arithmetic, local(): mass_after = jnp.sum(tracer_new * regridded_depths, axis=(1, 2, 3))  9.08 us
    ppermute x4, starting transfers between devices, passed_along(): return lax.ppermute(value, axis, pairs)  8.92 us
    slice x14, local copies, waits for them, and re-layouts, shifted_layers(): return jnp.concatenate([filler, values[..., :layers + amount, :]], axis=-2)  5.98 us
    concatenate x12, other arithmetic, ppm_parts(): jnp.concatenate([top_edge, second_edge, inner_edge, lower_edge, bottom_ed...  4.34 us
    reduce_sum x1, other arithmetic, local(): jnp.sum(0.5 * (regridded_depths + jnp.concatenate([regridded_depths[:, :,...  3.64 us
    slice x9, local copies, waits for them, and re-layouts, shifted_layers(): return jnp.concatenate([values[..., amount:, :], filler], axis=-2)  3.48 us
  transfers between devices with their start and end apart: 4, of which 1 were waited for; matrix products, arithmetic and copies ran while one was open for 34% of the time, Pallas kernels for 0%

profile of v1, /device:TPU:1, one launch (start us, length us, event | category | flops | bytes accessed | tf_op | source)
XLA Modules:
  0.0 134.6 jit_solution(13448924127715643606)
XLA Ops:
  0.6 1.7 %slice.551 = f32[2,120,1]{2,1,0:T(8,128)} slice(f32[2,120,128]{2,1,0:T(8,128)} %param.10), slice={[0:2], [0:120], [127:128]} | slice | bytes 1920 | tf_op jit(solution)/shard_map/slice | solution.py:176
  2.3 3.6 %collective-permute-start.2 = (f32[2,120,1]{2,1,0:T(8,128)}, f32[2,120,1]{2,1,0:T(8,128)}, u32[]{:S(2)}, u32[]{:S(2)}) collective-permute-start(f32[2,120,1]{2,1,0:T(8,128)} %slice.551), channel_id=1, source_target_pairs={{0,32},{32,64},{64,96},{96,128},{128,160},{160,192},{192,224},{224... | collective-permute-start | bytes 2888 | tf_op jit(solution)/shard_map/ppermute | solution.py:17
  5.9 0.6 fusion.103
  6.5 1.2 collective-permute-start
  7.8 1.0 copy-done.2
  9.5 1.1 fusion.7
  10.5 1.0 slice.631
  11.5 2.0 %fusion.86 = (f32[8,2,118,128]{3,2,1,0:T(8,128)}, f32[8,2,118,128]{3,2,1,0:T(8,128)}, f32[8,2,118,128]{3,2,1,0:T(8,128)}, f32[8,2,118,128]{3,2,1,0:T(8,128)}) fusion(f32[8,2,120,128]{3,2,1,0:T(8,128)S(1)} %get-tuple-element.65, f32[8,2,120,128]{3,2,1,0:T(8,128)S(1)} %get-tuple-element.66), kind=kLoop, calls=%fused_computation.223 | loop fusion | bytes 7733248 | tf_op jit(solution)/shard_map/slice | solution.py:56
  13.6 2.0 %fusion.87 = (f32[8,2,119,128]{3,2,1,0:T(8,128)}, f32[8,2,119,128]{3,2,1,0:T(8,128)}, f32[8,2,119,128]{3,2,1,0:T(8,128)}, f32[8,2,119,128]{3,2,1,0:T(8,128)}) fusion(f32[8,2,120,128]{3,2,1,0:T(8,128)S(1)} %get-tuple-element.65, f32[8,2,120,128]{3,2,1,0:T(8,128)S(1)} %get-tuple-element.66), kind=kLoop, calls=%fused_computation.224 | loop fusion | bytes 7798784 | tf_op jit(solution)/shard_map/slice | solution.py:56
  15.6 1.1 slice.626
  16.7 1.1 fusion
  17.7 1.0 pad_maximum_fusion.2
  18.8 0.8 copy-done.1
  19.7 1.3 fusion.46
  21.0 1.2 fusion.51
  22.1 0.6 slice_reduce_fusion
  22.8 0.8 slice.715
  23.5 0.7 fusion.102
  24.2 0.6 slice_bitcast_fusion.8
  25.0 0.5 copy-done.55
  25.5 0.7 fusion.61
  26.3 0.7 slice.709
  26.9 0.8 fusion.98
  27.7 0.8 fusion.99
  28.5 0.7 slice.704
  29.2 0.7 fusion.40
  29.9 0.7 pad_maximum_fusion.20
  30.5 0.7 pad_maximum_fusion.21
  31.2 1.3 dynamic-slice
  33.9 0.7 dynamic-slice.1
  35.9 1.3 dynamic-slice.2
  38.5 1.2 dynamic-slice.3
  40.9 1.3 dynamic-slice.4
  42.2 9.1 %multiply_reduce_fusion = (f32[8]{0:T(128)}, f32[8,2,120,128]{3,2,1,0:T(8,128)}) fusion(f32[2,120,128]{2,1,0:T(8,128)S(1)} %get-tuple-element.137, f32[2,120,128]{2,1,0:T(8,128)} %get-tuple-element.153, f32[2,120,128]{2,1,0:T(8,128)} %get-tuple-element.152, pred[2,120,128]{2,1,0:T(8,128)(4,1)S(1)} %get-tuple-element.139, ...), kind=kLoop, calls=%fused_computation.18 | loop fusion | flops 24084472 | bytes 17244192 | tf_op jit(solution)/shard_map/reduce_sum | solution.py:211
  53.3 0.6 copy-done.59
  54.0 0.7 copy-done.58
  55.6 1.0 maximum_bitcast_fusion.1
  57.3 0.6 copy-done.12
  58.4 1.0 add_divide_fusion.1
  59.5 0.8 slice.718
  60.2 0.6 copy-done.57
  60.9 3.8 %collective-permute-start.3 = (f32[3,2,120,1]{2,1,3,0:T(2,128)S(1)}, f32[3,2,120,1]{2,1,3,0:T(2,128)S(1)}, u32[]{:S(2)}, u32[]{:S(2)}) collective-permute-start(f32[3,2,120,1]{2,1,3,0:T(2,128)S(1)} %pad_maximum_fusion.23), channel_id=1, source_target_pairs={{0,224},{32,0},{64,32},{96,64},{128,96},{160,128},{192,160},{224,1... | collective-permute-start | bytes 8648 | tf_op jit(solution)/shard_map/ppermute | solution.py:17
  64.7 0.8 maximum_bitcast_fusion
  66.1 1.0 add_divide_fusion.2
  67.1 0.6 slice_bitcast_fusion.4
  68.0 0.4 collective-permute-start.1
  68.4 0.8 copy.187
  69.2 0.8 copy.188
  70.2 0.7 fusion.47
  71.6 1.5 %collective-permute-done.1 = f32[3,1,120,128]{3,2,1,0:T(8,128)S(1)} collective-permute-done((f32[3,1,120,128]{3,2,1,0:T(8,128)S(1)}, f32[3,1,120,128]{3,2,1,0:T(8,128)S(1)}, u32[]{:S(2)}, u32[]{:S(2)}) %collective-permute-start.1) | collective-permute-done | bytes 184352 | tf_op jit(solution)/shard_map/ppermute | solution.py:17
  73.1 0.6 copy-done.44
  73.9 0.5 copy-done.50
  74.4 3.6 %fusion.49 = (f32[]{:T(128)}, f32[]{:T(128)}, f32[]{:T(128)}, f32[]{:T(128)}, f32[2,120,128]{2,1,0:T(8,128)}, /*index=5*/f32[2,120,128]{2,1,0:T(8,128)}, f32[2,120,128]{2,1,0:T(8,128)}) fusion(f32[2,120,128]{2,1,0:T(8,128)S(1)} %get-tuple-element.137, f32[2,120,1]{2,1,0:T(8,128)} %copy.187, f32[2,120,127]{2,1,0:T(8,128)S(1)} %copy-done.31, ...), kind=kLoop, calls=%fused_computation.136 | loop fusion | flops 3839996 | bytes 3906576 | tf_op jit(solution)/shard_map/reduce_sum | solution.py:201
  80.1 1.5 %fusion.63 = (f32[]{:T(128)}, f32[]{:T(128)}) fusion(f32[3,1,120,128]{3,2,1,0:T(8,128)} %copy-done.44, f32[2,120,128]{2,1,0:T(8,128)S(1)} %copy-done, f32[2,120,128]{2,1,0:T(8,128)S(1)} %copy-done.5), kind=kLoop, calls=%fused_computation.176 | loop fusion | flops 153598 | bytes 307208 | tf_op jit(solution)/shard_map/reduce_sum | solution.py:163
  83.0 0.8 maximum_dynamic-update-slice_fusion
  83.8 7.5 %all-reduce.81 = (f32[32]{0:T(128)S(1)}, f32[32]{0:T(128)S(1)}, f32[12]{0:T(128)S(1)}) all-reduce(f32[32]{0:T(128)S(1)} %dynamic-update-slice, f32[32]{0:T(128)S(1)} %dynamic-update-slice.5, f32[12]{0:T(128)S(1)} %maximum_dynamic-update-slice_fusion), channel_id=2, replica_groups=mesh['gx_0'=4,'gx_1'=2,'gy_0'=8,'gy_1'=2,'gy_2'=2] {'gx_0'}, use_global_device_ids=true, to_apply=%add.65 | all-reduce | flops 76 | bytes 608
  92.3 5.3 %all-reduce.84 = (f32[16]{0:T(128)S(1)}, f32[16]{0:T(128)S(1)}, f32[6]{0:T(128)S(1)}) all-reduce(f32[16]{0:T(128)S(1)} %dynamic-update-slice.1, f32[16]{0:T(128)S(1)} %dynamic-update-slice.6, f32[6]{0:T(128)S(1)} %dynamic-update-slice.11), channel_id=3, replica_groups=mesh['gx_0'=4,'gx_1'=2,'gy_0'=8,'gy_1'=2,'gy_2'=2] {'gx_1'}, use_global_device_ids=true, to_apply=%add.66 | all-reduce | flops 38 | bytes 304
  98.5 16.5 %all-reduce.80 = (f32[64]{0:T(128)S(1)}, f32[64]{0:T(128)S(1)}, f32[24]{0:T(128)S(1)}) all-reduce(f32[64]{0:T(128)S(1)} %dynamic-update-slice.2, f32[64]{0:T(128)S(1)} %dynamic-update-slice.7, f32[24]{0:T(128)S(1)} %dynamic-update-slice.12), channel_id=4, replica_groups=mesh['gx_0'=4,'gx_1'=2,'gy_0'=8,'gy_1'=2,'gy_2'=2] {'gy_0'}, use_global_device_ids=true, to_apply=%add.67 | all-reduce | flops 152 | bytes 1216
  116.0 3.9 %all-reduce.83 = (f32[16]{0:T(128)S(1)}, f32[16]{0:T(128)S(1)}, f32[6]{0:T(128)S(1)}) all-reduce(f32[16]{0:T(128)S(1)} %dynamic-update-slice.3, f32[16]{0:T(128)S(1)} %dynamic-update-slice.8, f32[6]{0:T(128)S(1)} %dynamic-update-slice.13), channel_id=5, replica_groups=mesh['gx_0'=4,'gx_1'=2,'gy_0'=8,'gy_1'=2,'gy_2'=2] {'gy_1'}, use_global_device_ids=true, to_apply=%add.68 | all-reduce | flops 38 | bytes 304
  120.9 8.5 %all-reduce.82 = (f32[16]{0:T(128)S(1)}, f32[16]{0:T(128)S(1)}, f32[6]{0:T(128)S(1)}) all-reduce(f32[16]{0:T(128)S(1)} %dynamic-update-slice.4, f32[16]{0:T(128)S(1)} %dynamic-update-slice.9, f32[6]{0:T(128)S(1)} %dynamic-update-slice.14), channel_id=6, replica_groups=mesh['gx_0'=4,'gx_1'=2,'gy_0'=8,'gy_1'=2,'gy_2'=2] {'gy_2'}, use_global_device_ids=true, to_apply=%add.69 | all-reduce | flops 38 | bytes 304
  129.6 0.6 fusion.106
  130.9 0.6 subtract_divide_fusion
  131.6 1.1 broadcast_add_fusion
  134.0 0.7 broadcast_add_fusion.1
  (220 shorter events, 7.8 us)
Async XLA Ops:
  0.6 5.3 %copy-start.5 = (f32[2,120,128]{2,1,0:T(8,128)S(1)}, f32[2,120,128]{2,1,0:T(8,128)}, u32[]{:S(2)}) copy-start(f32[2,120,128]{2,1,0:T(8,128)} %param.9) | copy-start | bytes 368644
  2.3 5.4 %copy-start = (f32[2,120,128]{2,1,0:T(8,128)S(1)}, f32[2,120,128]{2,1,0:T(8,128)}, u32[]{:S(2)}) copy-start(f32[2,120,128]{2,1,0:T(8,128)} %param.12) | copy-start | bytes 368644
  2.3 53.3 %collective-permute-start.2 = (f32[2,120,1]{2,1,0:T(8,128)}, f32[2,120,1]{2,1,0:T(8,128)}, u32[]{:S(2)}, u32[]{:S(2)}) collective-permute-start(f32[2,120,1]{2,1,0:T(8,128)} %slice.551), channel_id=1, source_target_pairs={{0,32},{32,64},{64,96},{96,128},{128,160},{160,192},{192,224},{224... | collective-permute-start | bytes 2888 | tf_op jit(solution)/shard_map/ppermute | solution.py:17
  6.5 58.2 %collective-permute-start = (f32[1,120,128]{2,1,0:T(8,128)}, f32[1,120,128]{2,1,0:T(8,128)}, u32[]{:S(2)}, u32[]{:S(2)}) collective-permute-start(f32[1,120,128]{2,1,0:T(8,128)} %get-tuple-element.129), channel_id=1, source_target_pairs={{0,1},{1,2},{2,3},{3,4},{4,5},{5,6},{6,7},{7,8},{8,9},{9,10},{10,1... | collective-permute-start | bytes 184328 | tf_op jit(solution)/shard_map/ppermute | solution.py:17
  7.7 1.0 copy-start.2
  8.9 0.6 copy-start.48
  8.9 9.9 %copy-start.45 = (f32[8,2,1,128]{3,2,1,0:T(1,128)}, f32[8,2,1,128]{3,2,1,0:T(1,128)S(1)}, u32[]{:S(2)}) copy-start(f32[8,2,1,128]{3,2,1,0:T(1,128)S(1)} %get-tuple-element.78) | copy-start | bytes 24580
  18.7 0.9 copy-start.1
  19.6 1.3 copy-start.41
  19.7 1.3 copy-start.43
  19.7 1.3 copy-start.47
  23.5 1.3 copy-start.4
  24.9 4.9 %copy-start.49 = (f32[2,1,128]{2,1,0:T(1,128)}, f32[2,1,128]{2,1,0:T(1,128)S(1)}, u32[]{:S(2)}) copy-start(f32[2,1,128]{2,1,0:T(1,128)S(1)} %get-tuple-element.114) | copy-start | bytes 3076
  25.0 5.6 %copy-start.51 = (f32[2,1,128]{2,1,0:T(1,128)}, f32[2,1,128]{2,1,0:T(1,128)S(1)}, u32[]{:S(2)}) copy-start(f32[2,1,128]{2,1,0:T(1,128)S(1)} %get-tuple-element.112) | copy-start | bytes 3076
  25.0 5.6 %copy-start.53 = (f32[2,1,128]{2,1,0:T(1,128)}, f32[2,1,128]{2,1,0:T(1,128)S(1)}, u32[]{:S(2)}) copy-start(f32[2,1,128]{2,1,0:T(1,128)S(1)} %get-tuple-element.115) | copy-start | bytes 3076
  33.2 0.7 copy-start.60
  34.5 7.7 %copy-start.46 = (f32[8,2,1,128]{3,2,1,0:T(1,128)S(1)}, f32[8,2,1,128]{3,2,1,0:T(1,128)}, u32[]{:S(2)}) copy-start(f32[8,2,1,128]{3,2,1,0:T(1,128)} %copy-done.45) | copy-start | bytes 24580
  37.8 4.3 %copy-start.11 = (pred[2,120,128]{2,1,0:T(8,128)(4,1)S(1)}, pred[2,120,128]{2,1,0:T(8,128)(4,1)}, u32[]{:S(2)}) copy-start(pred[2,120,128]{2,1,0:T(8,128)(4,1)} %get-tuple-element.142) | copy-start | bytes 92164
  37.8 4.3 %copy-start.14 = (pred[2,120,128]{2,1,0:T(8,128)(4,1)S(1)}, pred[2,120,128]{2,1,0:T(8,128)(4,1)}, u32[]{:S(2)}) copy-start(pred[2,120,128]{2,1,0:T(8,128)(4,1)} %get-tuple-element.143) | copy-start | bytes 92164
  51.3 4.3 %copy-start.37 = (f32[2,120,127]{2,1,0:T(8,128)S(1)}, f32[2,120,127]{2,1,0:T(8,128)}, u32[]{:S(2)}) copy-start(f32[2,120,127]{2,1,0:T(8,128)} %get-tuple-element.118) | copy-start | bytes 365764
  53.2 0.6 copy-start.59
  54.0 0.7 copy-start.58
  57.1 0.8 copy-start.12
  57.1 0.8 copy-start.15
  57.1 0.8 copy-start.17
  57.1 0.8 copy-start.19
  57.2 0.8 copy-start.21
  57.2 0.8 copy-start.23
  57.2 0.8 copy-start.25
  57.2 0.8 copy-start.27
  57.2 0.8 copy-start.29
  57.2 1.0 copy-start.6
  57.2 1.0 copy-start.7
  57.3 1.1 copy-start.8
  57.3 1.1 copy-start.9
  59.5 5.2 %copy-start.40 = (f32[1,120,128]{2,1,0:T(8,128)S(1)}, f32[1,120,128]{2,1,0:T(8,128)}, u32[]{:S(2)}) copy-start(f32[1,120,128]{2,1,0:T(8,128)} %get-tuple-element.130) | copy-start | bytes 184324
  60.2 0.6 copy-start.57
  60.9 7.5 %collective-permute-start.3 = (f32[3,2,120,1]{2,1,3,0:T(2,128)S(1)}, f32[3,2,120,1]{2,1,3,0:T(2,128)S(1)}, u32[]{:S(2)}, u32[]{:S(2)}) collective-permute-start(f32[3,2,120,1]{2,1,3,0:T(2,128)S(1)} %pad_maximum_fusion.23), channel_id=1, source_target_pairs={{0,224},{32,0},{64,32},{96,64},{128,96},{160,128},{192,160},{224,1... | collective-permute-start | bytes 8648 | tf_op jit(solution)/shard_map/ppermute | solution.py:17
  67.1 0.8 copy-start.38
  67.1 0.9 copy-start.39
  68.0 5.7 %copy-start.33 = (f32[2,118,128]{2,1,0:T(8,128)S(1)}, f32[2,118,128]{2,1,0:T(8,128)}, u32[]{:S(2)}) copy-start(f32[2,118,128]{2,1,0:T(8,128)} %get-tuple-element.119) | copy-start | bytes 362500
  68.0 5.7 %copy-start.34 = (f32[2,118,128]{2,1,0:T(8,128)S(1)}, f32[2,118,128]{2,1,0:T(8,128)}, u32[]{:S(2)}) copy-start(f32[2,118,128]{2,1,0:T(8,128)} %get-tuple-element.120) | copy-start | bytes 362500
  68.0 5.7 %copy-start.35 = (f32[2,118,128]{2,1,0:T(8,128)S(1)}, f32[2,118,128]{2,1,0:T(8,128)}, u32[]{:S(2)}) copy-start(f32[2,118,128]{2,1,0:T(8,128)} %get-tuple-element.168) | copy-start | bytes 362500
  68.0 5.0 %collective-permute-start.1 = (f32[3,1,120,128]{3,2,1,0:T(8,128)S(1)}, f32[3,1,120,128]{3,2,1,0:T(8,128)S(1)}, u32[]{:S(2)}, u32[]{:S(2)}) collective-permute-start(f32[3,1,120,128]{3,2,1,0:T(8,128)S(1)} %pad_maximum_fusion.17), channel_id=1, source_target_pairs={{0,31},{1,0},{2,1},{3,2},{4,3},{5,4},{6,5},{7,6},{8,7},{9,8},{10,9... | collective-permute-start | bytes 552968 | tf_op jit(solution)/shard_map/ppermute | solution.py:17
  70.0 3.8 %copy-start.31 = (f32[2,120,127]{2,1,0:T(8,128)S(1)}, f32[2,120,127]{2,1,0:T(8,128)}, u32[]{:S(2)}) copy-start(f32[2,120,127]{2,1,0:T(8,128)} %slice.715) | copy-start | bytes 365764
  70.0 3.8 %copy-start.32 = (f32[2,117,128]{2,1,0:T(8,128)S(1)}, f32[2,117,128]{2,1,0:T(8,128)}, u32[]{:S(2)}) copy-start(f32[2,117,128]{2,1,0:T(8,128)} %slice.709) | copy-start | bytes 359428
  70.0 3.8 %copy-start.42 = (bf16[2,120,128]{2,1,0:T(8,128)(2,1)S(1)}, bf16[2,120,128]{2,1,0:T(8,128)(2,1)}, u32[]{:S(2)}) copy-start(bf16[2,120,128]{2,1,0:T(8,128)(2,1)} %param.14) | copy-start | bytes 184324
  70.1 3.7 %copy-start.22 = (pred[2,120,128]{2,1,0:T(8,128)(4,1)S(1)}, pred[2,120,128]{2,1,0:T(8,128)(4,1)}, u32[]{:S(2)}) copy-start(pred[2,120,128]{2,1,0:T(8,128)(4,1)} %get-tuple-element.147) | copy-start | bytes 92164
  70.1 3.7 %copy-start.24 = (pred[2,120,128]{2,1,0:T(8,128)(4,1)S(1)}, pred[2,120,128]{2,1,0:T(8,128)(4,1)}, u32[]{:S(2)}) copy-start(pred[2,120,128]{2,1,0:T(8,128)(4,1)} %get-tuple-element.148) | copy-start | bytes 92164
  70.1 3.7 %copy-start.26 = (pred[2,120,128]{2,1,0:T(8,128)(4,1)S(1)}, pred[2,120,128]{2,1,0:T(8,128)(4,1)}, u32[]{:S(2)}) copy-start(pred[2,120,128]{2,1,0:T(8,128)(4,1)} %get-tuple-element.149) | copy-start | bytes 92164
  70.1 3.7 %copy-start.28 = (pred[2,120,128]{2,1,0:T(8,128)(4,1)S(1)}, pred[2,120,128]{2,1,0:T(8,128)(4,1)}, u32[]{:S(2)}) copy-start(pred[2,120,128]{2,1,0:T(8,128)(4,1)} %get-tuple-element.150) | copy-start | bytes 92164
  70.2 3.7 %copy-start.30 = (pred[2,120,128]{2,1,0:T(8,128)(4,1)S(1)}, pred[2,120,128]{2,1,0:T(8,128)(4,1)}, u32[]{:S(2)}) copy-start(pred[2,120,128]{2,1,0:T(8,128)(4,1)} %get-tuple-element.151) | copy-start | bytes 92164
  70.2 3.7 %copy-start.52 = (f32[2,1,128]{2,1,0:T(1,128)S(1)}, f32[2,1,128]{2,1,0:T(1,128)}, u32[]{:S(2)}) copy-start(f32[2,1,128]{2,1,0:T(1,128)} %copy-done.51) | copy-start | bytes 3076
  70.2 3.7 %copy-start.54 = (f32[2,1,128]{2,1,0:T(1,128)S(1)}, f32[2,1,128]{2,1,0:T(1,128)}, u32[]{:S(2)}) copy-start(f32[2,1,128]{2,1,0:T(1,128)} %copy-done.53) | copy-start | bytes 3076
  70.2 3.7 %copy-start.56 = (f32[2,1,128]{2,1,0:T(1,128)S(1)}, f32[2,1,128]{2,1,0:T(1,128)}, u32[]{:S(2)}) copy-start(f32[2,1,128]{2,1,0:T(1,128)} %copy-done.55) | copy-start | bytes 3076
  71.6 2.3 %copy-start.10 = (f32[2,119,128]{2,1,0:T(8,128)S(1)}, f32[2,119,128]{2,1,0:T(8,128)}, u32[]{:S(2)}) copy-start(f32[2,119,128]{2,1,0:T(8,128)} %pad_maximum_fusion.21) | copy-start | bytes 365572
  73.1 0.7 copy-start.44
  73.1 0.8 copy-start.13
  73.1 0.8 copy-start.16
  73.1 0.8 copy-start.18
  73.1 0.9 copy-start.20
  73.7 0.7 copy-start.50
  74.4 57.1 %copy-start.3 = (f32[8,2,120,128]{3,2,1,0:T(8,128)S(1)}, f32[8,2,120,128]{3,2,1,0:T(8,128)}, u32[]{:S(2)}) copy-start(f32[8,2,120,128]{3,2,1,0:T(8,128)} %get-tuple-element.49) | copy-start | bytes 2949124
  131.5 2.4 %copy-start.36 = (f32[2,120,128]{2,1,0:T(8,128)S(1)}, f32[2,120,128]{2,1,0:T(8,128)}, u32[]{:S(2)}) copy-start(f32[2,120,128]{2,1,0:T(8,128)} %get-tuple-element.33) | copy-start | bytes 368644
  (1 other events, 0.6 us)
